TPU v7x, 32 devices: a whole 2x2x4 slice. The times are simulated.
32 devices in a mesh: samp: 8 (over z, core), var: 4 (over y, x).
Axes of the slice: x: 2, y: 2, z: 4, core: 2. Of those that a mesh axis runs over, the one named last changes fastest.
Arguments:
- hap_words: int32 [2, 512, 512], P(None, 'samp', 'var'), may hold values from 0 to 1073741823
- total_counts: int32 [15360, 8192], P('samp', 'var'), may hold values from 0 to 4999
- allele_one: int32 [15360, 8192], P('samp', 'var'), may hold values from 0 to 299
- allele_two: int32 [15360, 8192], P('samp', 'var'), may hold values from 0 to 299
Outputs:
- z_total: float32 [512, 8192], P('samp', 'var')
- z_allelic: float32 [512, 8192], P('samp', 'var')
Inputs may be any that keep to these rules, and one draw needn't show every extreme that they name: Bit k, for k below 30, of hap_words[c, j, v] is haplotype c of sample 30 * j + k at variant v; higher bits are zero.
All inputs are finite; a program needn't handle non-finite values.
Results may differ from a plain program's by a relative error of at most 0.0003.
The roundings to bfloat16 on the way count: a program that leaves them out, or rounds other values in their place, can miss the bound.
Values sent between devices are 32-bit elements; how exact they have to be, the bound alone decides.
A program may use at most 192 MiB of HBM per device.

v0:
```python
import jax
import jax.numpy as jnp
from jax import lax
from jax.sharding import PartitionSpec as P

BITS = 30


def unpack(packed):
    shifts = jnp.arange(BITS, dtype=jnp.int32)
    bit_table = jnp.bitwise_and(
        jnp.right_shift(packed[:, :, None, :], shifts[None, None, :, None]), 1
    )
    return bit_table.reshape(2, packed.shape[1] * BITS, packed.shape[2])


def features(total_part, one_part, two_part):
    log_total = jnp.log1p(total_part.astype(jnp.float32))
    one_plus = one_part.astype(jnp.float32) + 1.0
    two_plus = two_part.astype(jnp.float32) + 1.0
    log_ratio = jnp.log(one_plus / two_plus)
    weight = 1.0 / (1.0 / one_plus + 1.0 / two_plus)
    return (log_total, (weight * log_ratio).astype(jnp.bfloat16), weight.astype(jnp.bfloat16))


def finish(pair_sums, dos_margin, gene_margin, sample_count):
    dos_sum, dos_sq = (dos_margin[0], dos_margin[1])
    gene_sum, gene_sq = (gene_margin[0], gene_margin[1])
    dosage_var = dos_sq - dos_sum * dos_sum / sample_count
    gene_var = gene_sq - gene_sum * gene_sum / sample_count
    covariance = pair_sums[0] - dos_sum[:, None] * gene_sum[None, :] / sample_count
    z_total = (
        jnp.sqrt(sample_count)
        * covariance
        / jnp.sqrt((dosage_var[:, None] + 1.0) * (gene_var[None, :] + 1.0))
    )
    z_allelic = pair_sums[1] / jnp.sqrt(pair_sums[2] + 1.0)
    return (z_total, z_allelic)


def gather_words(hap_words):
    size = lax.axis_size("var")
    here = lax.axis_index("var")
    blocks = [hap_words]
    for shift in range(1, size):
        blocks.append(
            lax.ppermute(hap_words, "var", [((i + shift) % size, i) for i in range(size)])
        )
    placed = []
    for owner in range(size):
        steps = lax.rem(owner - here + size, size)
        block = blocks[0]
        for shift in range(1, size):
            block = jnp.where(steps == shift, blocks[shift], block)
        placed.append(block)
    return jnp.concatenate(placed, axis=2)


def dosage_table(packed):
    bits = unpack(packed)
    dosage_b = (bits[0] + bits[1] - 1).astype(jnp.bfloat16)
    margin = jnp.stack(
        [
            jnp.sum(dosage_b, axis=0, dtype=jnp.float32),
            jnp.sum(dosage_b * dosage_b, axis=0, dtype=jnp.float32),
        ]
    )
    return (dosage_b, margin)


def phase_tables(packed):
    bits = unpack(packed)
    phase = bits[0] - bits[1]
    return (phase.astype(jnp.bfloat16), (phase * phase).astype(jnp.bfloat16))


def pair_sum(table, feature):
    return jnp.einsum("sv,sg->vg", table, feature, preferred_element_type=jnp.float32)


def per_device(hap_words, total_counts, allele_one, allele_two):
    groups = lax.axis_size("samp")
    me = lax.axis_index("samp")
    core = lax.rem(me, 2)
    swap = [(i, i ^ 1) for i in range(groups)]
    halves = [list(range(c, groups, 2)) for c in (0, 1)]

    def scattered(chip_sum):
        return lax.psum_scatter(
            chip_sum, "samp", scatter_dimension=0, axis_index_groups=halves, tiled=True
        )

    def chip_sums(sent_table, kept_table, feature):
        partner = lax.ppermute(pair_sum(sent_table, feature), "samp", swap)
        return partner + lax.optimization_barrier(pair_sum(kept_table, feature))

    words = gather_words(hap_words)
    log_total = jnp.log1p(total_counts.astype(jnp.float32))
    gene_margin = jnp.stack([jnp.sum(log_total, axis=0), jnp.sum(log_total * log_total, axis=0)])
    total_b = log_total.astype(jnp.bfloat16)
    total_b, gene_margin = lax.optimization_barrier((total_b, gene_margin))

    width = words.shape[2] // groups
    split = words.reshape(2, words.shape[1], groups // 2, 2, width)
    flat = (2, words.shape[1], groups // 2 * width)
    low, high = (split[:, :, :, 0].reshape(flat), split[:, :, :, 1].reshape(flat))
    sent_words = jnp.where(core == 0, high, low)
    kept_words = jnp.where(core == 0, low, high)
    sent_dos, sent_margin = dosage_table(sent_words)
    kept_dos, kept_margin = dosage_table(kept_words)

    sent_total = pair_sum(sent_dos, total_b)
    kept_total = lax.optimization_barrier(pair_sum(kept_dos, total_b))
    chip_total = lax.ppermute(sent_total, "samp", swap) + kept_total
    chip_total, allele_one, allele_two, sent_words, kept_words = lax.optimization_barrier(
        (chip_total, allele_one, allele_two, sent_words, kept_words)
    )
    own_total = scattered(chip_total)
    sent_phase, sent_sq = phase_tables(sent_words)
    kept_phase, kept_sq = phase_tables(kept_words)

    _, weighted_b, weight_b = features(total_counts, allele_one, allele_two)
    weighted_b, weight_b = lax.optimization_barrier((weighted_b, weight_b))
    own_allelic = scattered(chip_sums(sent_phase, kept_phase, weighted_b))
    own_het = scattered(chip_sums(sent_sq, kept_sq, weight_b))

    parts = (2, groups // 2, width)
    even = jnp.where(core == 0, kept_margin, sent_margin).reshape(parts)
    odd = jnp.where(core == 0, sent_margin, kept_margin).reshape(parts)
    dos_margin = jnp.stack([even, odd], axis=2).reshape(2, groups * width)
    margins = jnp.concatenate([gene_margin, dos_margin], axis=1)
    margins, own_total = lax.optimization_barrier((margins, own_total))
    margins = lax.psum(margins, "samp")
    genes = gene_margin.shape[1]
    own_dos = lax.dynamic_slice_in_dim(margins, genes + me * width, width, axis=1)
    sample_count = jnp.float32(hap_words.shape[1] * BITS * groups)
    return finish(
        (own_total, own_allelic, own_het), own_dos, margins[:, :genes], sample_count
    )


def solution(mesh):
    in_specs = (P(None, "samp", "var"), P("samp", "var"), P("samp", "var"), P("samp", "var"))
    out_specs = (P("samp", "var"), P("samp", "var"))
    return jax.shard_map(
        per_device, mesh=mesh, in_specs=in_specs, out_specs=out_specs, check_vma=False
    )
```

profile of v0, /device:TPU:0, one launch (start us, length us, event | category | flops | bytes accessed | tf_op | source)
XLA Modules:
  0.0 189.5 jit_solution(10633935239728044843)
XLA Ops:
  7.2 0.0 reduce-scatter.4.cloned.1.call-start
  7.2 3.1 %collective-permute-start.1 = (s32[2,64,128]{2,1,0:T(8,128)}, s32[2,64,128]{2,1,0:T(8,128)S(1)}, u32[]{:S(2)}, u32[]{:S(2)}) collective-permute-start(s32[2,64,128]{2,1,0:T(8,128)} %param.4), channel_id=1, source_target_pairs={{2,0},{3,1},{0,2},{1,3},{6,4},{7,5},{4,6},{5,7},{10,8},{11,9},{8,1... | collective-permute-start | bytes 196616 | tf_op jit(solution)/shard_map/ppermute | solution.py:47
  10.3 1.5 collective-permute-start
  11.8 1.4 collective-permute-start.2
  13.2 11.9 %fusion = (f32[2048]{0:T(1024)S(1)}, f32[2048]{0:T(1024)S(1)}, bf16[1920,2048]{1,0:T(8,128)(2,1)}) fusion(s32[1920,2048]{1,0:T(8,128)} %param.5), kind=kLoop, calls=%fused_computation.6 | loop fusion | flops 19656704 | bytes 23609344 | tf_op jit(solution)/shard_map/reduce_sum | solution.py:99
  25.2 0.4 reshape.203
  25.6 1.7 fusion.8
  27.3 0.2 select_n.158
  27.5 0.6 shift-right-arithmetic_and_fusion.2
  28.2 0.7 convert_reduce_fusion
  28.8 0.3 convert_element_type.82
  29.1 6.9 %fusion.16 = f32[256,2048]{1,0:T(8,128)} fusion(bf16[1920,256]{1,0:T(8,128)(2,1)S(1)} %convert_element_type.82, bf16[1920,2048]{1,0:T(8,128)(2,1)} %get-tuple-element.14), kind=kOutput, calls=%fused_computation.56 | convolution fusion | flops 2013265920 | bytes 10944512 | tf_op jit(solution)/shard_map/sv,sg->vg/dot_general | solution.py:78
  36.0 0.2 select_n.156
  36.2 0.6 shift-right-arithmetic_and_fusion.3
  36.8 0.7 convert_reduce_fusion.2
  37.5 0.3 convert_element_type.83
  37.8 5.6 %fusion.17 = f32[256,2048]{1,0:T(8,128)S(1)} fusion(bf16[1920,256]{1,0:T(8,128)(2,1)S(1)} %convert_element_type.83, bf16[1920,2048]{1,0:T(8,128)(2,1)} %get-tuple-element.14), kind=kOutput, calls=%fused_computation.57 | convolution fusion | flops 2013265920 | bytes 10944512 | tf_op jit(solution)/shard_map/sv,sg->vg/dot_general | solution.py:78
  43.4 3.3 %add.98 = f32[256,2048]{1,0:T(8,128)} add(f32[256,2048]{1,0:T(8,128)} %collective-permute-done.3, f32[256,2048]{1,0:T(8,128)S(1)} %fusion.17) | non-fusion elementwise | flops 524288 | bytes 6291456 | tf_op jit(solution)/shard_map/add | solution.py:114
  46.7 0.0 reduce-scatter.4.cloned.1.call-update
  46.7 0.2 reduce-scatter.8.cloned.1.call-start
  46.9 17.8 %fusion.12 = (bf16[1920,2048]{1,0:T(8,128)(2,1)}, bf16[1920,2048]{1,0:T(8,128)(2,1)}) fusion(s32[1920,2048]{1,0:T(8,128)} %param.7, s32[1920,2048]{1,0:T(8,128)} %param.6), kind=kLoop, calls=%fused_computation.54 | loop fusion | flops 47185920 | bytes 47185920 | tf_op jit(solution)/shard_map/convert_element_type | solution.py:23
  64.7 2.7 %shift-right-arithmetic_and_fusion = (s32[2,64,30,256]{3,2,1,0:T(8,128)}, s32[2,64,30,256]{3,2,1,0:T(8,128)S(1)}) fusion(s32[2,64,256]{2,1,0:T(8,128)S(1)} %select_n.156, s32[2,64,256]{2,1,0:T(8,128)S(1)} %select_n.158), kind=kLoop, calls=%fused_computation.8 | loop fusion | flops 3932160 | bytes 8126464 | tf_op jit(solution)/shard_map/and | solution.py:11
  67.4 0.7 multiply_convert_fusion.2
  68.1 0.3 convert_element_type.93
  68.3 7.2 %fusion.20 = f32[256,2048]{1,0:T(8,128)} fusion(bf16[1920,256]{1,0:T(8,128)(2,1)S(1)} %convert_element_type.93, bf16[1920,2048]{1,0:T(8,128)(2,1)} %get-tuple-element.23), kind=kOutput, calls=%fused_computation.60 | convolution fusion | flops 2013265920 | bytes 10944512 | tf_op jit(solution)/shard_map/sv,sg->vg/dot_general | solution.py:78
  75.5 0.7 collective-permute-start.5
  76.2 1.7 multiply_convert_fusion.1
  77.8 1.4 convert_element_type.95
  79.2 5.6 %fusion.21 = f32[256,2048]{1,0:T(8,128)S(1)} fusion(bf16[1920,256]{1,0:T(8,128)(2,1)S(1)} %convert_element_type.95, bf16[1920,2048]{1,0:T(8,128)(2,1)} %get-tuple-element.23), kind=kOutput, calls=%fused_computation.61 | convolution fusion | flops 2013265920 | bytes 10944512 | tf_op jit(solution)/shard_map/sv,sg->vg/dot_general | solution.py:78
  84.9 3.3 %add.108 = f32[256,2048]{1,0:T(8,128)} add(f32[256,2048]{1,0:T(8,128)} %collective-permute-done.5, f32[256,2048]{1,0:T(8,128)S(1)} %fusion.21) | non-fusion elementwise | flops 524288 | bytes 6291456 | tf_op jit(solution)/shard_map/add | solution.py:95
  88.2 0.0 reduce-scatter.8.cloned.1.call-update
  88.2 0.3 reduce-scatter.6.cloned.1.call-start
  88.5 0.3 convert_element_type.85
  88.7 7.0 %fusion.18 = f32[256,2048]{1,0:T(8,128)} fusion(bf16[1920,256]{1,0:T(8,128)(2,1)S(1)} %convert_element_type.85, bf16[1920,2048]{1,0:T(8,128)(2,1)} %get-tuple-element.21), kind=kOutput, calls=%fused_computation.58 | convolution fusion | flops 2013265920 | bytes 10944512 | tf_op jit(solution)/shard_map/sv,sg->vg/dot_general | solution.py:78
  95.8 0.3 convert_element_type.91
  96.0 6.0 %fusion.19 = f32[256,2048]{1,0:T(8,128)S(1)} fusion(bf16[1920,256]{1,0:T(8,128)(2,1)S(1)} %convert_element_type.91, bf16[1920,2048]{1,0:T(8,128)(2,1)} %get-tuple-element.21), kind=kOutput, calls=%fused_computation.59 | convolution fusion | flops 2013265920 | bytes 10944512 | tf_op jit(solution)/shard_map/sv,sg->vg/dot_general | solution.py:78
  102.0 3.3 %add.107 = f32[256,2048]{1,0:T(8,128)} add(f32[256,2048]{1,0:T(8,128)} %collective-permute-done.4, f32[256,2048]{1,0:T(8,128)S(1)} %fusion.19) | non-fusion elementwise | flops 524288 | bytes 6291456 | tf_op jit(solution)/shard_map/add | solution.py:95
  105.3 0.1 stack.37
  105.4 0.1 stack.36
  105.5 0.1 stack.34
  105.6 0.1 stack.33
  105.7 0.1 reshape.204
  105.8 0.0 reduce-scatter.4.cloned.1.call-done
  105.8 31.5 %psum.7 = f32[2,2560]{1,0:T(2,128)S(1)} all-reduce(f32[2,2560]{1,0:T(2,128)S(1)} %pad_maximum_fusion), channel_id=1, replica_groups=mesh['samp'=8,'var'=4] {'samp'}, use_global_device_ids=true, to_apply=%region_7.8 | all-reduce | flops 5120 | bytes 40960 | tf_op jit(solution)/shard_map/psum | solution.py:133
  137.4 0.1 constant_dynamic-slice_fusion
  137.5 2.1 %rsqrt_multiply_fusion.1 = f32[64,2048]{1,0:T(8,128)} fusion(f32[64,2048]{1,0:T(8,128)} %reduce-scatter.4.cloned.1.call-done, f32[2048]{0:T(1024)S(1)} %bitcast.27, f32[64]{0:T(128)S(1)} %fusion.11, f32[2048]{0:T(1024)S(1)} %bitcast.26, f32[64]{0:T(128)S(1)} %slice_bitcast_fusion), kind=kLoop, calls=%fused_computation.29 | loop fusion | flops 786432 | bytes 1065472 | tf_op jit(solution)/shard_map/div | solution.py:33
  139.5 41.4 %reduce-scatter.6.cloned.1.call-done = f32[64,2048]{1,0:T(8,128)} async-done(((f32[256,2048]{1,0:T(8,128)}), f32[64,2048]{1,0:T(8,128)}) %reduce-scatter.6.cloned.1.call-update) | async-done | bytes 524304 | tf_op jit(solution)/shard_map/reduce_scatter | solution.py:89
  180.9 2.1 %rsqrt_multiply_fusion = f32[64,2048]{1,0:T(8,128)} fusion(f32[64,2048]{1,0:T(8,128)} %reduce-scatter.6.cloned.1.call-done, f32[64,2048]{1,0:T(8,128)} %reduce-scatter.8.cloned.1.call-done), kind=kLoop, calls=%fused_computation.28 | loop fusion | flops 262144 | bytes 1572864 | tf_op jit(solution)/shard_map/div | solution.py:37
  (26 shorter events, 0.2 us)
Async XLA Ops:
  7.2 18.0 %copy-start.1 = (s32[2,64,128]{2,1,0:T(8,128)S(1)}, s32[2,64,128]{2,1,0:T(8,128)}, u32[]{:S(2)}) copy-start(s32[2,64,128]{2,1,0:T(8,128)} %param.4) | copy-start | bytes 196612
  7.2 98.7 %reduce-scatter.4.cloned.1.call-start = ((), (), s32[]{:S(2)}) async-start(), calls=%async_computation.3 | async-start | bytes 2621440 | tf_op jit(solution)/shard_map/reduce_scatter | solution.py:89
  7.2 17.9 %collective-permute-start.1 = (s32[2,64,128]{2,1,0:T(8,128)}, s32[2,64,128]{2,1,0:T(8,128)S(1)}, u32[]{:S(2)}, u32[]{:S(2)}) collective-permute-start(s32[2,64,128]{2,1,0:T(8,128)} %param.4), channel_id=1, source_target_pairs={{2,0},{3,1},{0,2},{1,3},{6,4},{7,5},{4,6},{5,7},{10,8},{11,9},{8,1... | collective-permute-start | bytes 196616 | tf_op jit(solution)/shard_map/ppermute | solution.py:47
  10.3 14.9 %collective-permute-start = (s32[2,64,128]{2,1,0:T(8,128)}, s32[2,64,128]{2,1,0:T(8,128)S(1)}, u32[]{:S(2)}, u32[]{:S(2)}) collective-permute-start(s32[2,64,128]{2,1,0:T(8,128)} %param.4), channel_id=1, source_target_pairs={{3,0},{0,1},{1,2},{2,3},{7,4},{4,5},{5,6},{6,7},{11,8},{8,9},{9,10... | collective-permute-start | bytes 196616 | tf_op jit(solution)/shard_map/ppermute | solution.py:47
  11.8 13.4 %collective-permute-start.2 = (s32[2,64,128]{2,1,0:T(8,128)}, s32[2,64,128]{2,1,0:T(8,128)S(1)}, u32[]{:S(2)}, u32[]{:S(2)}) collective-permute-start(s32[2,64,128]{2,1,0:T(8,128)} %param.4), channel_id=1, source_target_pairs={{1,0},{2,1},{3,2},{0,3},{5,4},{6,5},{7,6},{4,7},{9,8},{10,9},{11,1... | collective-permute-start | bytes 196616 | tf_op jit(solution)/shard_map/ppermute | solution.py:47
  36.0 7.4 %collective-permute-start.3 = (f32[256,2048]{1,0:T(8,128)}, f32[256,2048]{1,0:T(8,128)}, u32[]{:S(2)}, u32[]{:S(2)}) collective-permute-start(f32[256,2048]{1,0:T(8,128)} %fusion.16), channel_id=1, source_target_pairs={{0,4},{4,0},{8,12},{12,8},{16,20},{20,16},{24,28},{28,24},{1,5},{5... | collective-permute-start | bytes 6291464 | tf_op jit(solution)/shard_map/ppermute | solution.py:114
  46.7 92.8 %reduce-scatter.8.cloned.1.call-start = ((), (), s32[]{:S(2)}) async-start(), calls=%async_computation.5 | async-start | bytes 2621440 | tf_op jit(solution)/shard_map/reduce_scatter | solution.py:89
  68.3 7.8 %copy-start = (s32[2,64,30,256]{3,2,1,0:T(8,128)S(1)}, s32[2,64,30,256]{3,2,1,0:T(8,128)}, u32[]{:S(2)}) copy-start(s32[2,64,30,256]{3,2,1,0:T(8,128)} %get-tuple-element.51) | copy-start | bytes 11796484
  75.5 9.3 %collective-permute-start.5 = (f32[256,2048]{1,0:T(8,128)}, f32[256,2048]{1,0:T(8,128)}, u32[]{:S(2)}, u32[]{:S(2)}) collective-permute-start(f32[256,2048]{1,0:T(8,128)} %fusion.20), channel_id=1, source_target_pairs={{0,4},{4,0},{8,12},{12,8},{16,20},{20,16},{24,28},{28,24},{1,5},{5... | collective-permute-start | bytes 6291464 | tf_op jit(solution)/shard_map/ppermute | solution.py:94
  88.2 92.8 %reduce-scatter.6.cloned.1.call-start = ((), (), s32[]{:S(2)}) async-start(), calls=%async_computation.4 | async-start | bytes 2621440 | tf_op jit(solution)/shard_map/reduce_scatter | solution.py:89
  95.8 6.3 %collective-permute-start.4 = (f32[256,2048]{1,0:T(8,128)}, f32[256,2048]{1,0:T(8,128)}, u32[]{:S(2)}, u32[]{:S(2)}) collective-permute-start(f32[256,2048]{1,0:T(8,128)} %fusion.18), channel_id=1, source_target_pairs={{0,4},{4,0},{8,12},{12,8},{16,20},{20,16},{24,28},{28,24},{1,5},{5... | collective-permute-start | bytes 6291464 | tf_op jit(solution)/shard_map/ppermute | solution.py:94
Sparse Core Ops, SparseCore 0:
  46.8 43.1 reduce-scatter.3
  92.3 43.3 reduce-scatter.7
  138.0 42.8 reduce-scatter.5
where the time goes:
time: 190 us
  other arithmetic  53.1 us (28%)
  waiting for transfers between devices  41.5 us (22%)
  matrix products  38.3 us (20%)
  blocking collectives  31.5 us (17%)
  between operations  14 us (7%)
  starting transfers between devices  7.17 us (4%)
  local copies, waits for them, and re-layouts  3.98 us (2%)
    reduce_scatter x3, waiting for transfers between devices, scattered(): lax.psum_scatter(chip_sum, 'samp', scatter_dimension=0, axis_index_groups...  41.4 us
    dot_general x6, matrix products, pair_sum(): jnp.einsum('sv,sg->vg', table, feature, preferred_element_type=jnp.float32)  38.3 us
    psum x1, blocking collectives, per_device(): margins = lax.psum(margins, 'samp')  31.5 us
    convert_element_type x1, other arithmetic, features(): weight.astype(jnp.bfloat16)  17.8 us
    reduce_sum x1, other arithmetic, per_device(): jnp.sum(log_total, axis=0)  11.9 us
    add x2, other arithmetic, chip_sums(): return partner + lax.optimization_barrier(pair_sum(kept_table, feature))  6.6 us
    ppermute x3, starting transfers between devices, gather_words(): lax.ppermute(hap_words, 'var', [((i + shift) % size, i) for i in range(si...  5.99 us
    and x3, other arithmetic, unpack(): jnp.bitwise_and(jnp.right_shift(packed[:, :, None, :], shifts[None, None,...  3.99 us
  transfers between devices with their start and end apart: 9, of which 1 were waited for; matrix products, arithmetic and copies ran while one was open for 42% of the time, Pallas kernels for 0%

commit v1 on v0

v1 whole, which is shorter than its diff:
```python
import functools
import math

import jax
import jax.numpy as jnp
from jax import lax
from jax.experimental import pallas as pl
from jax.experimental.pallas import tpu as pltpu
from jax.sharding import PartitionSpec as P

BITS = 30
TILE = 256
CHUNK = 128
MESH = pl.DeviceIdType.MESH


def kernel(
    chips,
    owners,
    early,
    hap_ref,
    total_ref,
    one_ref,
    two_ref,
    z_total_ref,
    z_allelic_ref,
    words,
    nat,
    tables,
    inputs,
    feats,
    own,
    swapped,
    arrived,
    margins,
    word_send,
    word_recv,
    word_local,
    in_sem,
    swap_send,
    swap_recv,
    hop_send,
    hop_recv,
    margin_send,
    margin_recv,
):
    me = lax.axis_index("samp")
    group = lax.axis_index("var")
    place = lax.div(me, 2)
    core = lax.rem(me, 2)
    partner = me + 1 - 2 * core
    word_rows, block = words.shape[2], words.shape[3]
    samples = tables.shape[2]
    tiles = own.shape[0]
    rows = own.shape[4]
    sample_count = float(samples * 2 * chips)

    def fetch(tile, slot):
        columns = pl.ds(pl.multiple_of(tile * TILE, TILE), TILE)
        return [
            pltpu.make_async_copy(
                ref.at[:, columns], inputs.at[slot, kind], in_sem.at[slot, kind]
            )
            for kind, ref in enumerate((total_ref, one_ref, two_ref))
        ]

    for copy in fetch(0, 0):
        copy.start()
    local = pltpu.make_async_copy(hap_ref, words.at[group], word_local)
    local.start()

    barrier = pltpu.get_barrier_semaphore()
    pl.semaphore_signal(barrier, inc=1, device_id={"samp": partner}, device_id_type=MESH)

    @pl.when(place > 0)
    def _():
        pl.semaphore_signal(barrier, inc=1, device_id={"samp": me - 2}, device_id_type=MESH)

    @pl.when(place < chips - 1)
    def _():
        pl.semaphore_signal(barrier, inc=1, device_id={"samp": me + 2}, device_id_type=MESH)

    for shift in range(1, owners):
        other = lax.rem(group + shift, owners)
        pl.semaphore_signal(barrier, inc=1, device_id={"var": other}, device_id_type=MESH)
    inner = jnp.where(jnp.logical_and(place > 0, place < chips - 1), 1, 0)
    pl.semaphore_wait(barrier, owners + 1 + inner)

    def word_copy(shift):
        return pltpu.make_async_remote_copy(
            src_ref=hap_ref,
            dst_ref=words.at[group],
            send_sem=word_send.at[shift],
            recv_sem=word_recv.at[shift],
            device_id={"var": lax.rem(group + shift, owners)},
            device_id_type=MESH,
        )

    for shift in range(1, owners):
        word_copy(shift).start()

    def swap_copy(tile):
        return pltpu.make_async_remote_copy(
            src_ref=own.at[tile, :, :, 1 - core],
            dst_ref=swapped.at[tile],
            send_sem=swap_send.at[tile],
            recv_sem=swap_recv.at[tile],
            device_id={"samp": partner},
            device_id_type=MESH,
        )

    def hop_copy(tile, target, slot, toward):
        return pltpu.make_async_remote_copy(
            src_ref=arrived.at[tile, target],
            dst_ref=arrived.at[tile, slot],
            send_sem=hop_send.at[tile, target],
            recv_sem=hop_recv.at[tile, slot],
            device_id={"samp": toward},
            device_id_type=MESH,
        )

    def compute_features(tile, slot):
        def step(index, sums):
            part = pl.ds(pl.multiple_of(index * CHUNK, CHUNK), CHUNK)
            log_total = jnp.log(inputs[slot, 0, part, :].astype(jnp.float32) + 1.0)
            feats[0, part, :] = log_total.astype(jnp.bfloat16)
            one = inputs[slot, 1, part, :].astype(jnp.float32) + 1.0
            two = inputs[slot, 2, part, :].astype(jnp.float32) + 1.0
            weight = (one * two) / (one + two)
            ratio = jnp.log(one) - jnp.log(two)
            feats[1, part, :] = (weight * ratio).astype(jnp.bfloat16)
            feats[2, part, :] = weight.astype(jnp.bfloat16)
            split = log_total.reshape(CHUNK // 8, 8, TILE)
            return (sums[0] + jnp.sum(split, axis=0), sums[1] + jnp.sum(split * split, axis=0))

        zero = jnp.zeros((8, TILE), jnp.float32)
        sums = lax.fori_loop(0, samples // CHUNK, step, (zero, zero))
        margins[0, tile, 0:1, :] = jnp.sum(sums[0], axis=0, keepdims=True)
        margins[0, tile, 1:2, :] = jnp.sum(sums[1], axis=0, keepdims=True)

    def build_tables():
        def step(owner, carry):
            first, second = words[owner, 0], words[owner, 1]
            for bit in range(BITS):
                low = jnp.bitwise_and(jnp.right_shift(first, bit), 1)
                high = jnp.bitwise_and(jnp.right_shift(second, bit), 1)
                spread = pl.ds(bit, word_rows, stride=BITS)
                nat[0, spread, :] = (low + high - 1).astype(jnp.float32)
                nat[1, spread, :] = (low - high).astype(jnp.float32)
            dosage = nat[0].T
            phase = nat[1].T
            part = pl.ds(pl.multiple_of(owner * block, block), block)
            tables[0, part, :] = dosage.astype(jnp.bfloat16)
            tables[1, part, :] = phase.astype(jnp.bfloat16)
            tables[2, part, :] = (phase * phase).astype(jnp.bfloat16)
            return carry

        lax.fori_loop(0, owners, step, 0)
        per_tile = TILE // block
        for owner in range(owners):
            first, second = words[owner, 0], words[owner, 1]
            count = lax.population_count(first) + lax.population_count(second)
            differ = lax.population_count(jnp.bitwise_xor(first, second))
            lanes = pl.ds((owner % per_tile) * block, block)
            place_of = tiles + owner // per_tile
            all_bits = float(BITS * word_rows)
            margins[0, place_of, 0:1, lanes] = (
                jnp.sum(count.astype(jnp.float32), axis=0, keepdims=True) - all_bits
            )
            margins[0, place_of, 1:2, lanes] = all_bits - jnp.sum(
                differ.astype(jnp.float32), axis=0, keepdims=True
            )

    def multiply(tile):
        for kind in range(3):
            product = jnp.dot(tables[kind], feats[kind], preferred_element_type=jnp.float32)
            own[tile, kind] = product.reshape(chips, 2, rows, TILE)

    def chip_part(tile, target):
        return own[tile, :, target, core] + swapped[tile, :, target]

    def forward(tile):
        swap_copy(tile).wait_recv()
        for step in range(chips - 1):
            far, near = chips - 1 - step, step

            @pl.when(far > place)
            def _():
                @pl.when(place > 0)
                def _():
                    hop_copy(tile, far, far, me - 2).wait_recv()
                    arrived[tile, far] = arrived[tile, far] + chip_part(tile, far)

                @pl.when(place == 0)
                def _():
                    arrived[tile, far] = chip_part(tile, far)

                hop_copy(tile, far, far, me + 2).start()

            @pl.when(near < place)
            def _():
                @pl.when(place < chips - 1)
                def _():
                    hop_copy(tile, near, near, me + 2).wait_recv()
                    arrived[tile, near] = arrived[tile, near] + chip_part(tile, near)

                @pl.when(place == chips - 1)
                def _():
                    arrived[tile, near] = chip_part(tile, near)

                slot = jnp.where(place - 1 == near, chips, near)
                hop_copy(tile, near, slot, me - 2).start()

    def drain(tile):
        swap_copy(tile).wait_send()
        for target in range(chips):

            @pl.when(target != place)
            def _():
                hop_copy(tile, target, target, partner).wait_send()

    def margin_copy(index, source, slot, toward):
        return pltpu.make_async_remote_copy(
            src_ref=margins.at[source],
            dst_ref=margins.at[slot],
            send_sem=margin_send.at[index],
            recv_sem=margin_recv.at[index],
            device_id={"samp": toward},
            device_id_type=MESH,
        )

    def reduce_margins():
        margin_copy(0, 0, 1, partner).wait_recv()
        margins[2] = margins[0] + margins[1]

        @pl.when(place == 0)
        def _():
            margins[5] = margins[2]

        @pl.when(place > 0)
        def _():
            margin_copy(1, 5, 3, me - 2).wait_recv()
            margins[5] = margins[2] + margins[3]

        @pl.when(place < chips - 1)
        def _():
            margin_copy(1, 5, 3, me + 2).start()

        @pl.when(place == chips - 1)
        def _():
            margins[4] = jnp.zeros_like(margins[4])
            margins[6] = margins[2]

        @pl.when(place < chips - 1)
        def _():
            margin_copy(2, 6, 4, me + 2).wait_recv()
            margins[6] = margins[2] + margins[4]

        @pl.when(place > 0)
        def _():
            margin_copy(2, 6, 4, me - 2).start()

    def own_column(kind):
        lane = lax.broadcasted_iota(jnp.int32, (rows, TILE), 1)
        row = lax.broadcasted_iota(jnp.int32, (rows, TILE), 0)
        column = jnp.zeros((rows, 1), jnp.float32)
        for piece in range(margins.shape[1] - tiles):
            whole = (
                margins[5, tiles + piece, kind : kind + 1, :]
                + margins[4, tiles + piece, kind : kind + 1, :]
            )
            hit = lane + piece * TILE == me * rows + row
            column = column + jnp.sum(jnp.where(hit, whole, 0.0), axis=1, keepdims=True)
        return column

    def finish(tile):
        own[tile, :, place, core] = chip_part(tile, place)

        @pl.when(place > 0)
        def _():
            hop_copy(tile, place, place, me - 2).wait_recv()
            own[tile, :, place, core] = own[tile, :, place, core] + arrived[tile, place]

        @pl.when(place < chips - 1)
        def _():
            hop_copy(tile, place, chips, me + 2).wait_recv()
            own[tile, :, place, core] = own[tile, :, place, core] + arrived[tile, chips]

        sums = own[tile, :, place, core]
        dos_sum, dos_sq = own_column(0), own_column(1)
        gene_sum, gene_sq = (
            margins[5, tile, kind : kind + 1, :] + margins[4, tile, kind : kind + 1, :]
            for kind in (0, 1)
        )
        dosage_var = dos_sq - dos_sum * dos_sum / sample_count
        gene_var = gene_sq - gene_sum * gene_sum / sample_count
        covariance = sums[0] - dos_sum * gene_sum / sample_count
        columns = pl.ds(pl.multiple_of(tile * TILE, TILE), TILE)
        z_total_ref[:, columns] = (
            math.sqrt(sample_count)
            * covariance
            / jnp.sqrt((dosage_var + 1.0) * (gene_var + 1.0))
        )
        z_allelic_ref[:, columns] = sums[1] / jnp.sqrt(sums[2] + 1.0)

    for copy in fetch(0, 0):
        copy.wait()
    if tiles > 1:
        for copy in fetch(1, 1):
            copy.start()
    compute_features(0, 0)
    local.wait()
    for shift in range(1, owners):
        word_copy(shift).wait()
    build_tables()
    multiply(0)
    swap_copy(0).start()

    def compute_step(tile, carry):
        slot = lax.rem(tile, 2)
        for copy in fetch(tile, slot):
            copy.wait()

        @pl.when(tile + 1 < tiles)
        def _():
            for copy in fetch(tile + 1, 1 - slot):
                copy.start()

        compute_features(tile, slot)
        multiply(tile)
        swap_copy(tile).start()

        @pl.when(lax.rem(tile, 2) == 1)
        def _():
            ready = lax.div(tile, 2)

            @pl.when(ready < early)
            def _():
                forward(ready)

        return carry

    lax.fori_loop(1, tiles, compute_step, 0)
    margin_copy(0, 0, 1, partner).start()

    def later_step(tile, carry):
        @pl.when(tile >= 2)
        def _():
            drain(tile - 2)

        forward(tile)

        @pl.when(tile == early)
        def _():
            reduce_margins()

        @pl.when(tile > early)
        def _():
            finish(tile - 1)

        return carry

    lax.fori_loop(early, tiles, later_step, 0)
    for tile in range(early):
        finish(tile)
    finish(tiles - 1)
    for tile in range(max(early - 2, 0)):
        drain(tile)
    drain(tiles - 2)
    drain(tiles - 1)
    margin_copy(0, 0, 1, partner).wait_send()

    @pl.when(place < chips - 1)
    def _():
        margin_copy(1, 5, 3, partner).wait_send()

    @pl.when(place > 0)
    def _():
        margin_copy(2, 6, 4, partner).wait_send()


def per_device(hap_words, total_counts, allele_one, allele_two):
    devices = lax.axis_size("samp")
    owners = lax.axis_size("var")
    chips = devices // 2
    samples, genes = total_counts.shape
    _, word_rows, block = hap_words.shape
    variants = block * owners
    rows = variants // devices
    tiles = genes // TILE
    early = min(3, tiles - 2)
    pieces = variants // TILE
    hbm = pl.BlockSpec(memory_space=pltpu.MemorySpace.HBM)
    vmem = pl.BlockSpec(memory_space=pltpu.MemorySpace.VMEM)
    out = jax.ShapeDtypeStruct((rows, genes), jnp.float32)
    dma = pltpu.SemaphoreType.DMA
    f32 = jnp.float32
    return pl.pallas_call(
        functools.partial(kernel, chips, owners, early),
        out_shape=(out, out),
        in_specs=[hbm] * 4,
        out_specs=(vmem, vmem),
        scratch_shapes=[
            pltpu.VMEM((owners, 2, word_rows, block), jnp.int32),
            pltpu.VMEM((2, samples, block), f32),
            pltpu.VMEM((3, variants, samples), jnp.bfloat16),
            pltpu.VMEM((2, 3, samples, TILE), jnp.int32),
            pltpu.VMEM((3, samples, TILE), jnp.bfloat16),
            pltpu.VMEM((tiles, 3, chips, 2, rows, TILE), f32),
            pltpu.VMEM((tiles, 3, chips, rows, TILE), f32),
            pltpu.VMEM((tiles, chips + 1, 3, rows, TILE), f32),
            pltpu.VMEM((7, tiles + pieces, 2, TILE), f32),
            dma((owners,)),
            dma((owners,)),
            dma,
            dma((2, 3)),
            dma((tiles,)),
            dma((tiles,)),
            dma((tiles, chips)),
            dma((tiles, chips + 1)),
            dma((3,)),
            dma((3,)),
        ],
        compiler_params=pltpu.CompilerParams(
            collective_id=0, has_side_effects=True, vmem_limit_bytes=67043328
        ),
    )(hap_words, total_counts, allele_one, allele_two)


def solution(mesh):
    in_specs = (P(None, "samp", "var"), P("samp", "var"), P("samp", "var"), P("samp", "var"))
    out_specs = (P("samp", "var"), P("samp", "var"))
    return jax.shard_map(
        per_device, mesh=mesh, in_specs=in_specs, out_specs=out_specs, check_vma=False
    )
```

time: 190 us -> 162 us (0.85)
  Pallas kernels: 0 us -> 157 us
  other arithmetic: 53.1 us -> 0 us
  waiting for transfers between devices: 41.5 us -> 0 us
  matrix products: 38.3 us -> 0 us
  blocking collectives: 31.5 us -> 0 us
  between operations: 14 us -> 0.64 us
  starting transfers between devices: 7.17 us -> 0 us
    pallas_call x0 -> x1, Pallas kernels: none -> 157 us  [per_device(): pl.pallas_call(functools.partial(kernel, chips, owners, early), out_shape...]
    reduce_scatter x3 -> x0, waiting for transfers between devices: 41.4 us -> none  [scattered(): lax.psum_scatter(chip_sum, 'samp', scatter_dimension=0, axis_index_groups...]
    dot_general x6 -> x0, matrix products: 38.3 us -> none  [pair_sum(): jnp.einsum('sv,sg->vg', table, feature, preferred_element_type=jnp.float32)]
    psum x1 -> x0, blocking collectives: 31.5 us -> none  [per_device(): margins = lax.psum(margins, 'samp')]
    convert_element_type x3 -> x0, other arithmetic: 20.1 us -> none  [the longest x1 17.8 us: features(): weight.astype(jnp.bfloat16)]
    reduce_sum x3 -> x0, other arithmetic: 13.2 us -> none  [the longest x1 11.9 us: per_device(): jnp.sum(log_total, axis=0)]
    add x4 -> x0, other arithmetic: 9.91 us -> none  [the longest x2 6.6 us: chip_sums(): return partner + lax.optimization_barrier(pair_sum(kept_table, feature))]
    ppermute x6 -> x0, starting transfers between devices: 6.65 us -> none  [the longest x3 5.99 us: gather_words(): lax.ppermute(hap_words, 'var', [((i + shift) % size, i) for i in range(si...]
  transfers between devices with their start and end apart: 9 -> 0, of which waited for: 1 -> 0; matrix products, arithmetic and copies ran while one was open for 42% -> 0% of each run, Pallas kernels for 0% -> 0%
where the time goes in v1:
time: 162 us; the launch traced here: 161 us
  Pallas kernels  157 us (97%)
  local copies, waits for them, and re-layouts  3.74 us (2%)
    pallas_call x1, Pallas kernels, per_device(): pl.pallas_call(functools.partial(kernel, chips, owners, early), out_shape...  157 us
    unnamed x2, local copies, waits for them, and re-layouts  3.74 us

profile of v1, /device:TPU:0, one launch (start us, length us, event | category | flops | bytes accessed | tf_op | source)
XLA Modules:
  0.0 161.3 jit_solution(18252068611305566654)
XLA Ops:
  0.6 156.9 %shard_map.59 = (f32[64,2048]{1,0:T(8,128)}, f32[64,2048]{1,0:T(8,128)}) custom-call(s32[2,64,128]{2,1,0:T(8,128)} %hap_ref.1, s32[1920,2048]{1,0:T(8,128)} %total_ref.1, s32[1920,2048]{1,0:T(8,128)} %one_ref.1, s32[1920,2048]{1,0:T(8,128)} %two_ref.1), custom_call_target="tpu_custom_call" | custom-call | tf_op jit(solution)/shard_map/pallas_call | solution.py:398
  157.5 1.9 %copy.8 = f32[64,2048]{1,0:T(8,128)} copy(f32[64,2048]{1,0:T(8,128)} %get-tuple-element.4) | data formatting | bytes 1048576
  159.4 1.9 %copy.9 = f32[64,2048]{1,0:T(8,128)} copy(f32[64,2048]{1,0:T(8,128)} %get-tuple-element.5) | data formatting | bytes 1048576

commit v2 on v1

--- a/solution.py
+++ b/solution.py
@@ -17,7 +17,6 @@
 def kernel(
     chips,
     owners,
-    early,
     hap_ref,
     total_ref,
     one_ref,
@@ -54,6 +53,10 @@
     tiles = own.shape[0]
     rows = own.shape[4]
     sample_count = float(samples * 2 * chips)
+    middle = jnp.logical_and(place > 0, place < chips - 1)
+    left_half = place < chips // 2
+    early = (tiles - 1) // 3
+    meet = max(tiles - 3, 1)
 
     def fetch(tile, slot):
         columns = pl.ds(pl.multiple_of(tile * TILE, TILE), TILE)
@@ -83,8 +86,7 @@
     for shift in range(1, owners):
         other = lax.rem(group + shift, owners)
         pl.semaphore_signal(barrier, inc=1, device_id={"var": other}, device_id_type=MESH)
-    inner = jnp.where(jnp.logical_and(place > 0, place < chips - 1), 1, 0)
-    pl.semaphore_wait(barrier, owners + 1 + inner)
+    pl.semaphore_wait(barrier, owners + 1 + jnp.where(middle, 1, 0))
 
     def word_copy(shift):
         return pltpu.make_async_remote_copy(
@@ -179,37 +181,32 @@
     def chip_part(tile, target):
         return own[tile, :, target, core] + swapped[tile, :, target]
 
+    def sweep(tile, rightward):
+        head = jnp.where(rightward, 0, chips - 1)
+        toward = jnp.where(rightward, me + 2, me - 2)
+        behind = jnp.where(rightward, me - 2, me + 2)
+        for step in range(chips - 1):
+            target = jnp.where(rightward, chips - 1 - step, step)
+            ahead = jnp.where(rightward, target - place, place - target)
+
+            @pl.when(ahead > 0)
+            def _():
+                @pl.when(place != head)
+                def _():
+                    hop_copy(tile, target, target, behind).wait_recv()
+                    arrived[tile, target] = arrived[tile, target] + chip_part(tile, target)
+
+                @pl.when(place == head)
+                def _():
+                    arrived[tile, target] = chip_part(tile, target)
+
+                last = jnp.logical_and(jnp.logical_not(rightward), ahead == 1)
+                hop_copy(tile, target, jnp.where(last, chips, target), toward).start()
+
     def forward(tile):
         swap_copy(tile).wait_recv()
-        for step in range(chips - 1):
-            far, near = chips - 1 - step, step
-
-            @pl.when(far > place)
-            def _():
-                @pl.when(place > 0)
-                def _():
-                    hop_copy(tile, far, far, me - 2).wait_recv()
-                    arrived[tile, far] = arrived[tile, far] + chip_part(tile, far)
-
-                @pl.when(place == 0)
-                def _():
-                    arrived[tile, far] = chip_part(tile, far)
-
-                hop_copy(tile, far, far, me + 2).start()
-
-            @pl.when(near < place)
-            def _():
-                @pl.when(place < chips - 1)
-                def _():
-                    hop_copy(tile, near, near, me + 2).wait_recv()
-                    arrived[tile, near] = arrived[tile, near] + chip_part(tile, near)
-
-                @pl.when(place == chips - 1)
-                def _():
-                    arrived[tile, near] = chip_part(tile, near)
-
-                slot = jnp.where(place - 1 == near, chips, near)
-                hop_copy(tile, near, slot, me - 2).start()
+        sweep(tile, left_half)
+        sweep(tile, jnp.logical_not(left_half))
 
     def drain(tile):
         swap_copy(tile).wait_send()
@@ -229,34 +226,39 @@
             device_id_type=MESH,
         )
 
-    def reduce_margins():
+    def start_margins():
+        margin_copy(0, 0, 1, partner).start()
         margin_copy(0, 0, 1, partner).wait_recv()
         margins[2] = margins[0] + margins[1]
 
         @pl.when(place == 0)
         def _():
+            margins[3] = jnp.zeros_like(margins[3])
             margins[5] = margins[2]
-
+            margin_copy(1, 5, 3, me + 2).start()
+
+        @pl.when(place == chips - 1)
+        def _():
+            margins[4] = jnp.zeros_like(margins[4])
+            margins[6] = margins[2]
+            margin_copy(2, 6, 4, me - 2).start()
+
+    def pass_margins():
         @pl.when(place > 0)
         def _():
             margin_copy(1, 5, 3, me - 2).wait_recv()
             margins[5] = margins[2] + margins[3]
 
-        @pl.when(place < chips - 1)
+        @pl.when(middle)
         def _():
             margin_copy(1, 5, 3, me + 2).start()
-
-        @pl.when(place == chips - 1)
-        def _():
-            margins[4] = jnp.zeros_like(margins[4])
-            margins[6] = margins[2]
 
         @pl.when(place < chips - 1)
         def _():
             margin_copy(2, 6, 4, me + 2).wait_recv()
             margins[6] = margins[2] + margins[4]
 
-        @pl.when(place > 0)
+        @pl.when(middle)
         def _():
             margin_copy(2, 6, 4, me - 2).start()
 
@@ -330,44 +332,44 @@
         multiply(tile)
         swap_copy(tile).start()
 
-        @pl.when(lax.rem(tile, 2) == 1)
-        def _():
-            ready = lax.div(tile, 2)
-
-            @pl.when(ready < early)
-            def _():
-                forward(ready)
+        @pl.when(jnp.logical_and(jnp.logical_not(middle), tile <= meet))
+        def _():
+            forward(tile - 1)
+
+        @pl.when(jnp.logical_and(middle, jnp.logical_and(lax.rem(tile, 3) == 0, tile <= 3 * early)))
+        def _():
+            forward(lax.div(tile, 3) - 1)
 
         return carry
 
+    def forward_step(tile, carry):
+        forward(tile)
+        return carry
+
+    def finish_step(tile, carry):
+        finish(tile)
+        return carry
+
+    def later_step(tile, carry):
+        @pl.when(middle)
+        def _():
+            forward(tile)
+
+        finish(tile - 1)
+        return carry
+
+    def drain_step(tile, carry):
+        drain(tile)
+        return carry
+
     lax.fori_loop(1, tiles, compute_step, 0)
-    margin_copy(0, 0, 1, partner).start()
-
-    def later_step(tile, carry):
-        @pl.when(tile >= 2)
-        def _():
-            drain(tile - 2)
-
-        forward(tile)
-
-        @pl.when(tile == early)
-        def _():
-            reduce_margins()
-
-        @pl.when(tile > early)
-        def _():
-            finish(tile - 1)
-
-        return carry
-
-    lax.fori_loop(early, tiles, later_step, 0)
-    for tile in range(early):
-        finish(tile)
+    start_margins()
+    lax.fori_loop(jnp.where(middle, early, meet), jnp.where(middle, meet + 1, tiles), forward_step, 0)
+    pass_margins()
+    lax.fori_loop(0, meet, finish_step, 0)
+    lax.fori_loop(meet + 1, tiles, later_step, 0)
     finish(tiles - 1)
-    for tile in range(max(early - 2, 0)):
-        drain(tile)
-    drain(tiles - 2)
-    drain(tiles - 1)
+    lax.fori_loop(0, tiles, drain_step, 0)
     margin_copy(0, 0, 1, partner).wait_send()
 
     @pl.when(place < chips - 1)
@@ -388,7 +390,6 @@
     variants = block * owners
     rows = variants // devices
     tiles = genes // TILE
-    early = min(3, tiles - 2)
     pieces = variants // TILE
     hbm = pl.BlockSpec(memory_space=pltpu.MemorySpace.HBM)
     vmem = pl.BlockSpec(memory_space=pltpu.MemorySpace.VMEM)
@@ -396,7 +397,7 @@
     dma = pltpu.SemaphoreType.DMA
     f32 = jnp.float32
     return pl.pallas_call(
-        functools.partial(kernel, chips, owners, early),
+        functools.partial(kernel, chips, owners),
         out_shape=(out, out),
         in_specs=[hbm] * 4,
         out_specs=(vmem, vmem),

time: 162 us -> 130 us (0.80)
  Pallas kernels: 157 us -> 125 us
    pallas_call x1, Pallas kernels: 157 us -> 125 us  [per_device(): pl.pallas_call(functools.partial(kernel, chips, owners), out_shape=(out,...]
where the time goes in v2:
time: 130 us
  Pallas kernels  125 us (96%)
  local copies, waits for them, and re-layouts  3.74 us (3%)
    pallas_call x1, Pallas kernels, per_device(): pl.pallas_call(functools.partial(kernel, chips, owners), out_shape=(out,...  125 us
    unnamed x2, local copies, waits for them, and re-layouts  3.74 us

profile of v2, /device:TPU:0, one launch (start us, length us, event | category | flops | bytes accessed | tf_op | source)
XLA Modules:
  0.0 129.9 jit_solution(2173701612882256540)
XLA Ops:
  0.6 125.5 %shard_map.59 = (f32[64,2048]{1,0:T(8,128)}, f32[64,2048]{1,0:T(8,128)}) custom-call(s32[2,64,128]{2,1,0:T(8,128)} %hap_ref.1, s32[1920,2048]{1,0:T(8,128)} %total_ref.1, s32[1920,2048]{1,0:T(8,128)} %one_ref.1, s32[1920,2048]{1,0:T(8,128)} %two_ref.1), custom_call_target="tpu_custom_call" | custom-call | tf_op jit(solution)/shard_map/pallas_call | solution.py:399
  126.1 1.9 %copy.8 = f32[64,2048]{1,0:T(8,128)} copy(f32[64,2048]{1,0:T(8,128)} %get-tuple-element.4) | data formatting | bytes 1048576
  128.0 1.9 %copy.9 = f32[64,2048]{1,0:T(8,128)} copy(f32[64,2048]{1,0:T(8,128)} %get-tuple-element.5) | data formatting | bytes 1048576

commit v3 on v2

--- a/solution.py
+++ b/solution.py
@@ -31,6 +31,8 @@
     own,
     swapped,
     arrived,
+    results,
+    returned,
     margins,
     word_send,
     word_recv,
@@ -40,6 +42,8 @@
     swap_recv,
     hop_send,
     hop_recv,
+    back_send,
+    back_recv,
     margin_send,
     margin_recv,
 ):
@@ -55,8 +59,7 @@
     sample_count = float(samples * 2 * chips)
     middle = jnp.logical_and(place > 0, place < chips - 1)
     left_half = place < chips // 2
-    early = (tiles - 1) // 3
-    meet = max(tiles - 3, 1)
+    meet = max(tiles // 2, 1)
 
     def fetch(tile, slot):
         columns = pl.ds(pl.multiple_of(tile * TILE, TILE), TILE)
@@ -83,41 +86,77 @@
     def _():
         pl.semaphore_signal(barrier, inc=1, device_id={"samp": me + 2}, device_id_type=MESH)
 
+    for far in range(2, chips // 2):
+        for toward in (2 * far, -2 * far):
+            near_end = place == (0 if toward > 0 else chips - 1)
+            from_end = place == (far if toward < 0 else chips - 1 - far)
+
+            @pl.when(jnp.logical_or(near_end, from_end))
+            def _():
+                pl.semaphore_signal(
+                    barrier, inc=1, device_id={"samp": me + toward}, device_id_type=MESH
+                )
+
     for shift in range(1, owners):
         other = lax.rem(group + shift, owners)
         pl.semaphore_signal(barrier, inc=1, device_id={"var": other}, device_id_type=MESH)
-    pl.semaphore_wait(barrier, owners + 1 + jnp.where(middle, 1, 0))
+    inner = jnp.logical_and(place >= 2, place < chips - 2)
+    greeted = jnp.where(middle, jnp.where(inner, 2, 1), chips // 2 - 2)
+    pl.semaphore_wait(barrier, owners + 1 + greeted)
+    local.wait()
+
+    def peer(shift):
+        other = group
+        for bit in (1 << place_of for place_of in range(owners.bit_length())):
+            if shift & bit:
+                other = other + bit - 2 * bit * lax.rem(lax.div(group, bit), 2)
+        return other
 
     def word_copy(shift):
         return pltpu.make_async_remote_copy(
-            src_ref=hap_ref,
+            src_ref=words.at[group],
             dst_ref=words.at[group],
             send_sem=word_send.at[shift],
             recv_sem=word_recv.at[shift],
-            device_id={"var": lax.rem(group + shift, owners)},
+            device_id={"var": peer(shift)},
             device_id_type=MESH,
         )
 
-    for shift in range(1, owners):
+    direct = [shift for shift in range(1, owners) if shift & (shift - 1) == 0]
+    routed = [shift for shift in range(1, owners) if shift & (shift - 1) != 0]
+    for shift in direct:
         word_copy(shift).start()
 
-    def swap_copy(tile):
+    def kinds(which):
+        return pl.ds(which, 1 + which)
+
+    def swap_copy(tile, which):
         return pltpu.make_async_remote_copy(
-            src_ref=own.at[tile, :, :, 1 - core],
-            dst_ref=swapped.at[tile],
-            send_sem=swap_send.at[tile],
-            recv_sem=swap_recv.at[tile],
+            src_ref=own.at[tile, kinds(which), :, 1 - core],
+            dst_ref=swapped.at[tile, kinds(which)],
+            send_sem=swap_send.at[tile, which],
+            recv_sem=swap_recv.at[tile, which],
             device_id={"samp": partner},
             device_id_type=MESH,
         )
 
-    def hop_copy(tile, target, slot, toward):
+    def hop_copy(tile, target, slot, toward, which):
         return pltpu.make_async_remote_copy(
-            src_ref=arrived.at[tile, target],
-            dst_ref=arrived.at[tile, slot],
-            send_sem=hop_send.at[tile, target],
-            recv_sem=hop_recv.at[tile, slot],
+            src_ref=arrived.at[tile, target, kinds(which)],
+            dst_ref=arrived.at[tile, slot, kinds(which)],
+            send_sem=hop_send.at[tile, target, which],
+            recv_sem=hop_recv.at[tile, slot, which],
             device_id={"samp": toward},
+            device_id_type=MESH,
+        )
+
+    def back_copy(tile, step, target):
+        return pltpu.make_async_remote_copy(
+            src_ref=results.at[tile, step],
+            dst_ref=returned.at[tile],
+            send_sem=back_send.at[tile, step],
+            recv_sem=back_recv.at[tile],
+            device_id={"samp": 2 * target + core},
             device_id_type=MESH,
         )
 
@@ -140,24 +179,22 @@
         margins[0, tile, 0:1, :] = jnp.sum(sums[0], axis=0, keepdims=True)
         margins[0, tile, 1:2, :] = jnp.sum(sums[1], axis=0, keepdims=True)
 
-    def build_tables():
-        def step(owner, carry):
-            first, second = words[owner, 0], words[owner, 1]
-            for bit in range(BITS):
-                low = jnp.bitwise_and(jnp.right_shift(first, bit), 1)
-                high = jnp.bitwise_and(jnp.right_shift(second, bit), 1)
-                spread = pl.ds(bit, word_rows, stride=BITS)
-                nat[0, spread, :] = (low + high - 1).astype(jnp.float32)
-                nat[1, spread, :] = (low - high).astype(jnp.float32)
-            dosage = nat[0].T
-            phase = nat[1].T
-            part = pl.ds(pl.multiple_of(owner * block, block), block)
-            tables[0, part, :] = dosage.astype(jnp.bfloat16)
-            tables[1, part, :] = phase.astype(jnp.bfloat16)
-            tables[2, part, :] = (phase * phase).astype(jnp.bfloat16)
-            return carry
-
-        lax.fori_loop(0, owners, step, 0)
+    def build_table(owner):
+        first, second = words[owner, 0], words[owner, 1]
+        for bit in range(BITS):
+            low = jnp.bitwise_and(jnp.right_shift(first, bit), 1)
+            high = jnp.bitwise_and(jnp.right_shift(second, bit), 1)
+            spread = pl.ds(bit, word_rows, stride=BITS)
+            nat[0, spread, :] = (low + high - 1).astype(jnp.float32)
+            nat[1, spread, :] = (low - high).astype(jnp.float32)
+        dosage = nat[0].T
+        phase = nat[1].T
+        part = pl.ds(pl.multiple_of(owner * block, block), block)
+        tables[0, part, :] = dosage.astype(jnp.bfloat16)
+        tables[1, part, :] = phase.astype(jnp.bfloat16)
+        tables[2, part, :] = (phase * phase).astype(jnp.bfloat16)
+
+    def sum_tables():
         per_tile = TILE // block
         for owner in range(owners):
             first, second = words[owner, 0], words[owner, 1]
@@ -173,48 +210,107 @@
                 differ.astype(jnp.float32), axis=0, keepdims=True
             )
 
-    def multiply(tile):
-        for kind in range(3):
-            product = jnp.dot(tables[kind], feats[kind], preferred_element_type=jnp.float32)
-            own[tile, kind] = product.reshape(chips, 2, rows, TILE)
-
-    def chip_part(tile, target):
-        return own[tile, :, target, core] + swapped[tile, :, target]
-
-    def sweep(tile, rightward):
+    def multiply(tile, kind):
+        product = jnp.dot(tables[kind], feats[kind], preferred_element_type=jnp.float32)
+        own[tile, kind] = product.reshape(chips, 2, rows, TILE)
+
+    def chip_part(tile, target, which):
+        return own[tile, kinds(which), target, core] + swapped[tile, kinds(which), target]
+
+    def hop(tile, target, rightward, which, last):
         head = jnp.where(rightward, 0, chips - 1)
         toward = jnp.where(rightward, me + 2, me - 2)
         behind = jnp.where(rightward, me - 2, me + 2)
+
+        @pl.when(place != head)
+        def _():
+            hop_copy(tile, target, target, behind, which).wait_recv()
+            arrived[tile, target, kinds(which)] = arrived[
+                tile, target, kinds(which)
+            ] + chip_part(tile, target, which)
+
+        @pl.when(place == head)
+        def _():
+            arrived[tile, target, kinds(which)] = chip_part(tile, target, which)
+
+        hop_copy(tile, target, jnp.where(last, chips, target), toward, which).start()
+
+    def sweep_total(tile, rightward):
         for step in range(chips - 1):
             target = jnp.where(rightward, chips - 1 - step, step)
             ahead = jnp.where(rightward, target - place, place - target)
 
             @pl.when(ahead > 0)
             def _():
-                @pl.when(place != head)
-                def _():
-                    hop_copy(tile, target, target, behind).wait_recv()
-                    arrived[tile, target] = arrived[tile, target] + chip_part(tile, target)
-
-                @pl.when(place == head)
-                def _():
-                    arrived[tile, target] = chip_part(tile, target)
-
                 last = jnp.logical_and(jnp.logical_not(rightward), ahead == 1)
-                hop_copy(tile, target, jnp.where(last, chips, target), toward).start()
-
-    def forward(tile):
-        swap_copy(tile).wait_recv()
-        sweep(tile, left_half)
-        sweep(tile, jnp.logical_not(left_half))
+                hop(tile, target, rightward, 0, last)
+
+    def sweep_allelic(tile, rightward):
+        sink = jnp.where(rightward, chips - 1, 0)
+
+        @pl.when(place != sink)
+        def _():
+            for step in range(chips // 2):
+                target = jnp.where(rightward, chips // 2 + step, chips // 2 - 1 - step)
+                hop(tile, target, rightward, 1, False)
+
+    def near(tile):
+        swap_copy(tile, 0).wait_recv()
+        swap_copy(tile, 1).wait_recv()
+        sweep_allelic(tile, left_half)
+        sweep_total(tile, left_half)
+
+    def far(tile):
+        sweep_allelic(tile, jnp.logical_not(left_half))
+        sweep_total(tile, jnp.logical_not(left_half))
+
+    def first_forward():
+        swap_copy(0, 0).wait_recv()
+        sweep_total(0, left_half)
+        swap_copy(0, 1).wait_recv()
+        sweep_allelic(0, left_half)
+
+    def settle(tile):
+        columns = pl.ds(pl.multiple_of(tile * TILE, TILE), TILE)
+        for step in range(chips // 2):
+            target = jnp.where(left_half, chips // 2 - 1 - step, chips // 2 + step)
+            behind = jnp.where(left_half, me + 2, me - 2)
+            hop_copy(tile, target, target, behind, 1).wait_recv()
+            sums = arrived[tile, target, kinds(1)] + chip_part(tile, target, 1)
+            value = sums[0] / jnp.sqrt(sums[1] + 1.0)
+            if step < chips // 2 - 1:
+                results[tile, step] = value
+                back_copy(tile, step, target).start()
+            else:
+                z_allelic_ref[:, columns] = value
+
+    def deliver(tile):
+        columns = pl.ds(pl.multiple_of(tile * TILE, TILE), TILE)
+        back_copy(tile, 0, place).wait_recv()
+        z_allelic_ref[:, columns] = returned[tile]
 
     def drain(tile):
-        swap_copy(tile).wait_send()
+        for which in range(2):
+            swap_copy(tile, which).wait_send()
         for target in range(chips):
 
             @pl.when(target != place)
             def _():
-                hop_copy(tile, target, target, partner).wait_send()
+                hop_copy(tile, target, target, partner, 0).wait_send()
+
+            sent = jnp.logical_or(
+                jnp.logical_and(target < chips // 2, place > 0),
+                jnp.logical_and(target >= chips // 2, place < chips - 1),
+            )
+
+            @pl.when(sent)
+            def _():
+                hop_copy(tile, target, target, partner, 1).wait_send()
+
+        @pl.when(jnp.logical_not(middle))
+        def _():
+            for step in range(chips // 2 - 1):
+                back_copy(tile, step, place).wait_send()
 
     def margin_copy(index, source, slot, toward):
         return pltpu.make_async_remote_copy(
@@ -243,24 +339,24 @@
             margins[6] = margins[2]
             margin_copy(2, 6, 4, me - 2).start()
 
-    def pass_margins():
-        @pl.when(place > 0)
+    def pass_margins(rightward):
+        @pl.when(jnp.logical_and(rightward, place > 0))
         def _():
             margin_copy(1, 5, 3, me - 2).wait_recv()
             margins[5] = margins[2] + margins[3]
 
-        @pl.when(middle)
-        def _():
-            margin_copy(1, 5, 3, me + 2).start()
-
-        @pl.when(place < chips - 1)
+            @pl.when(middle)
+            def _():
+                margin_copy(1, 5, 3, me + 2).start()
+
+        @pl.when(jnp.logical_and(jnp.logical_not(rightward), place < chips - 1))
         def _():
             margin_copy(2, 6, 4, me + 2).wait_recv()
             margins[6] = margins[2] + margins[4]
 
-        @pl.when(middle)
-        def _():
-            margin_copy(2, 6, 4, me - 2).start()
+            @pl.when(middle)
+            def _():
+                margin_copy(2, 6, 4, me - 2).start()
 
     def own_column(kind):
         lane = lax.broadcasted_iota(jnp.int32, (rows, TILE), 1)
@@ -276,19 +372,19 @@
         return column
 
     def finish(tile):
-        own[tile, :, place, core] = chip_part(tile, place)
+        own[tile, kinds(0), place, core] = chip_part(tile, place, 0)
 
         @pl.when(place > 0)
         def _():
-            hop_copy(tile, place, place, me - 2).wait_recv()
-            own[tile, :, place, core] = own[tile, :, place, core] + arrived[tile, place]
+            hop_copy(tile, place, place, me - 2, 0).wait_recv()
+            own[tile, 0, place, core] = own[tile, 0, place, core] + arrived[tile, place, 0]
 
         @pl.when(place < chips - 1)
         def _():
-            hop_copy(tile, place, chips, me + 2).wait_recv()
-            own[tile, :, place, core] = own[tile, :, place, core] + arrived[tile, chips]
-
-        sums = own[tile, :, place, core]
+            hop_copy(tile, place, chips, me + 2, 0).wait_recv()
+            own[tile, 0, place, core] = own[tile, 0, place, core] + arrived[tile, chips, 0]
+
+        cross_total = own[tile, 0, place, core]
         dos_sum, dos_sq = own_column(0), own_column(1)
         gene_sum, gene_sq = (
             margins[5, tile, kind : kind + 1, :] + margins[4, tile, kind : kind + 1, :]
@@ -296,27 +392,44 @@
         )
         dosage_var = dos_sq - dos_sum * dos_sum / sample_count
         gene_var = gene_sq - gene_sum * gene_sum / sample_count
-        covariance = sums[0] - dos_sum * gene_sum / sample_count
+        covariance = cross_total - dos_sum * gene_sum / sample_count
         columns = pl.ds(pl.multiple_of(tile * TILE, TILE), TILE)
         z_total_ref[:, columns] = (
             math.sqrt(sample_count)
             * covariance
             / jnp.sqrt((dosage_var + 1.0) * (gene_var + 1.0))
         )
-        z_allelic_ref[:, columns] = sums[1] / jnp.sqrt(sums[2] + 1.0)
-
+
+    for shift in direct:
+        word_copy(shift).wait_send()
+    for shift in routed:
+        word_copy(shift).start()
     for copy in fetch(0, 0):
         copy.wait()
     if tiles > 1:
         for copy in fetch(1, 1):
             copy.start()
     compute_features(0, 0)
-    local.wait()
-    for shift in range(1, owners):
-        word_copy(shift).wait()
-    build_tables()
-    multiply(0)
-    swap_copy(0).start()
+    build_table(group)
+    for shift in direct + routed:
+        word_copy(shift).wait_recv()
+        build_table(peer(shift))
+    for shift in routed:
+        word_copy(shift).wait_send()
+    multiply(0, 0)
+    swap_copy(0, 0).start()
+    for kind in (1, 2):
+        multiply(0, kind)
+    swap_copy(0, 1).start()
+
+    @pl.when(jnp.logical_not(middle))
+    def _():
+        first_forward()
+
+    sum_tables()
+
+    early = 2 if tiles >= 8 else 0
+    plan = ((3, near, 0), (5, far, 0), (6, near, 1), (7, far, 1))[: 2 * early]
 
     def compute_step(tile, carry):
         slot = lax.rem(tile, 2)
@@ -329,21 +442,37 @@
                 copy.start()
 
         compute_features(tile, slot)
-        multiply(tile)
-        swap_copy(tile).start()
-
-        @pl.when(jnp.logical_and(jnp.logical_not(middle), tile <= meet))
-        def _():
-            forward(tile - 1)
-
-        @pl.when(jnp.logical_and(middle, jnp.logical_and(lax.rem(tile, 3) == 0, tile <= 3 * early)))
-        def _():
-            forward(lax.div(tile, 3) - 1)
-
-        return carry
-
-    def forward_step(tile, carry):
-        forward(tile)
+        for kind in range(3):
+            multiply(tile, kind)
+        for which in range(2):
+            swap_copy(tile, which).start()
+
+        @pl.when(jnp.logical_and(jnp.logical_not(middle), jnp.logical_and(tile > 1, tile <= meet)))
+        def _():
+            near(tile - 1)
+
+        for due, sweep, which in plan:
+
+            @pl.when(jnp.logical_and(middle, tile == due))
+            def _():
+                sweep(which)
+
+        return carry
+
+    def near_step(tile, carry):
+        near(tile)
+        return carry
+
+    def both_step(tile, carry):
+        near(tile)
+        far(tile)
+        return carry
+
+    def settle_step(tile, carry):
+        @pl.when(jnp.logical_not(middle))
+        def _():
+            settle(tile)
+
         return carry
 
     def finish_step(tile, carry):
@@ -351,11 +480,17 @@
         return carry
 
     def later_step(tile, carry):
-        @pl.when(middle)
-        def _():
-            forward(tile)
-
+        @pl.when(jnp.logical_and(middle, tile < tiles))
+        def _():
+            near(tile)
+            far(tile)
+
+        settle_step(tile - 1, 0)
         finish(tile - 1)
+        return carry
+
+    def deliver_step(tile, carry):
+        deliver(tile)
         return carry
 
     def drain_step(tile, carry):
@@ -364,11 +499,26 @@
 
     lax.fori_loop(1, tiles, compute_step, 0)
     start_margins()
-    lax.fori_loop(jnp.where(middle, early, meet), jnp.where(middle, meet + 1, tiles), forward_step, 0)
-    pass_margins()
-    lax.fori_loop(0, meet, finish_step, 0)
-    lax.fori_loop(meet + 1, tiles, later_step, 0)
-    finish(tiles - 1)
+    lax.fori_loop(meet, jnp.where(middle, meet, tiles), near_step, 0)
+    lax.fori_loop(early, jnp.where(middle, meet + 1, early), both_step, 0)
+
+    @pl.when(middle)
+    def _():
+        pass_margins(left_half)
+        near(meet + 1)
+        far(meet + 1)
+        pass_margins(jnp.logical_not(left_half))
+
+    lax.fori_loop(0, meet, settle_step, 0)
+
+    @pl.when(jnp.logical_not(middle))
+    def _():
+        settle(meet)
+        pass_margins(jnp.logical_not(left_half))
+
+    lax.fori_loop(0, meet + 1, finish_step, 0)
+    lax.fori_loop(meet + 2, tiles + 1, later_step, 0)
+    lax.fori_loop(0, jnp.where(middle, tiles, 0), deliver_step, 0)
     lax.fori_loop(0, tiles, drain_step, 0)
     margin_copy(0, 0, 1, partner).wait_send()
 
@@ -410,15 +560,19 @@
             pltpu.VMEM((tiles, 3, chips, 2, rows, TILE), f32),
             pltpu.VMEM((tiles, 3, chips, rows, TILE), f32),
             pltpu.VMEM((tiles, chips + 1, 3, rows, TILE), f32),
+            pltpu.VMEM((tiles, max(chips // 2 - 1, 1), rows, TILE), f32),
+            pltpu.VMEM((tiles, rows, TILE), f32),
             pltpu.VMEM((7, tiles + pieces, 2, TILE), f32),
             dma((owners,)),
             dma((owners,)),
             dma,
             dma((2, 3)),
+            dma((tiles, 2)),
+            dma((tiles, 2)),
+            dma((tiles, chips, 2)),
+            dma((tiles, chips + 1, 2)),
+            dma((tiles, max(chips // 2 - 1, 1))),
             dma((tiles,)),
-            dma((tiles,)),
-            dma((tiles, chips)),
-            dma((tiles, chips + 1)),
             dma((3,)),
             dma((3,)),
         ],

time: 130 us -> 115 us (0.88)
  Pallas kernels: 125 us -> 111 us
    pallas_call x1, Pallas kernels: 125 us -> 111 us  [per_device(): pl.pallas_call(functools.partial(kernel, chips, owners), out_shape=(out,...]
where the time goes in v3:
time: 115 us
  Pallas kernels  111 us (97%)
  local copies, waits for them, and re-layouts  3.74 us (3%)
    pallas_call x1, Pallas kernels, per_device(): pl.pallas_call(functools.partial(kernel, chips, owners), out_shape=(out,...  111 us
    unnamed x2, local copies, waits for them, and re-layouts  3.74 us

profile of v3, /device:TPU:0, one launch (start us, length us, event | category | flops | bytes accessed | tf_op | source)
XLA Modules:
  0.0 115.0 jit_solution(3853111413789914751)
XLA Ops:
  0.6 110.6 %shard_map.59 = (f32[64,2048]{1,0:T(8,128)}, f32[64,2048]{1,0:T(8,128)}) custom-call(s32[2,64,128]{2,1,0:T(8,128)} %hap_ref.1, s32[1920,2048]{1,0:T(8,128)} %total_ref.1, s32[1920,2048]{1,0:T(8,128)} %one_ref.1, s32[1920,2048]{1,0:T(8,128)} %two_ref.1), custom_call_target="tpu_custom_call" | custom-call | tf_op jit(solution)/shard_map/pallas_call | solution.py:549
  111.2 1.9 %copy.8 = f32[64,2048]{1,0:T(8,128)} copy(f32[64,2048]{1,0:T(8,128)} %get-tuple-element.4) | data formatting | bytes 1048576
  113.1 1.9 %copy.9 = f32[64,2048]{1,0:T(8,128)} copy(f32[64,2048]{1,0:T(8,128)} %get-tuple-element.5) | data formatting | bytes 1048576

commit v4 on v3

--- a/solution.py
+++ b/solution.py
@@ -235,24 +235,33 @@
 
         hop_copy(tile, target, jnp.where(last, chips, target), toward, which).start()
 
+    def hop_total(tile, rightward, step):
+        target = jnp.where(rightward, chips - 1 - step, step)
+        ahead = jnp.where(rightward, target - place, place - target)
+
+        @pl.when(ahead > 0)
+        def _():
+            last = jnp.logical_and(jnp.logical_not(rightward), ahead == 1)
+            hop(tile, target, rightward, 0, last)
+
+    def hop_allelic(tile, rightward, step):
+        sink = jnp.where(rightward, chips - 1, 0)
+        target = jnp.where(rightward, chips // 2 + step, chips // 2 - 1 - step)
+
+        @pl.when(place != sink)
+        def _():
+            hop(tile, target, rightward, 1, False)
+
+    steps = [(hop_allelic, step) for step in range(chips // 2)]
+    steps += [(hop_total, step) for step in range(chips - 1)]
+
     def sweep_total(tile, rightward):
         for step in range(chips - 1):
-            target = jnp.where(rightward, chips - 1 - step, step)
-            ahead = jnp.where(rightward, target - place, place - target)
-
-            @pl.when(ahead > 0)
-            def _():
-                last = jnp.logical_and(jnp.logical_not(rightward), ahead == 1)
-                hop(tile, target, rightward, 0, last)
+            hop_total(tile, rightward, step)
 
     def sweep_allelic(tile, rightward):
-        sink = jnp.where(rightward, chips - 1, 0)
-
-        @pl.when(place != sink)
-        def _():
-            for step in range(chips // 2):
-                target = jnp.where(rightward, chips // 2 + step, chips // 2 - 1 - step)
-                hop(tile, target, rightward, 1, False)
+        for step in range(chips // 2):
+            hop_allelic(tile, rightward, step)
 
     def near(tile):
         swap_copy(tile, 0).wait_recv()
@@ -260,6 +269,13 @@
         sweep_allelic(tile, left_half)
         sweep_total(tile, left_half)
 
+    def near_and_far(ahead, behind):
+        swap_copy(ahead, 0).wait_recv()
+        swap_copy(ahead, 1).wait_recv()
+        for one_hop, step in steps:
+            one_hop(ahead, left_half, step)
+            one_hop(behind, jnp.logical_not(left_half), step)
+
     def far(tile):
         sweep_allelic(tile, jnp.logical_not(left_half))
         sweep_total(tile, jnp.logical_not(left_half))
@@ -270,7 +286,7 @@
         swap_copy(0, 1).wait_recv()
         sweep_allelic(0, left_half)
 
-    def settle(tile):
+    def settle(tile, send):
         columns = pl.ds(pl.multiple_of(tile * TILE, TILE), TILE)
         for step in range(chips // 2):
             target = jnp.where(left_half, chips // 2 - 1 - step, chips // 2 + step)
@@ -280,16 +296,22 @@
             value = sums[0] / jnp.sqrt(sums[1] + 1.0)
             if step < chips // 2 - 1:
                 results[tile, step] = value
-                back_copy(tile, step, target).start()
+                if send:
+                    back_copy(tile, step, target).start()
             else:
                 z_allelic_ref[:, columns] = value
+
+    def send_back(tile):
+        for step in range(chips // 2 - 1):
+            target = jnp.where(left_half, chips // 2 - 1 - step, chips // 2 + step)
+            back_copy(tile, step, target).start()
 
     def deliver(tile):
         columns = pl.ds(pl.multiple_of(tile * TILE, TILE), TILE)
         back_copy(tile, 0, place).wait_recv()
         z_allelic_ref[:, columns] = returned[tile]
 
-    def drain(tile):
+    def drain_hops(tile):
         for which in range(2):
             swap_copy(tile, which).wait_send()
         for target in range(chips):
@@ -307,10 +329,9 @@
             def _():
                 hop_copy(tile, target, target, partner, 1).wait_send()
 
-        @pl.when(jnp.logical_not(middle))
-        def _():
-            for step in range(chips // 2 - 1):
-                back_copy(tile, step, place).wait_send()
+    def drain_back(tile):
+        for step in range(chips // 2 - 1):
+            back_copy(tile, step, place).wait_send()
 
     def margin_copy(index, source, slot, toward):
         return pltpu.make_async_remote_copy(
@@ -429,7 +450,7 @@
     sum_tables()
 
     early = 2 if tiles >= 8 else 0
-    plan = ((3, near, 0), (5, far, 0), (6, near, 1), (7, far, 1))[: 2 * early]
+    plan = ((3, near, 0), (5, near, 1), (6, far, 0)) if early else ()
 
     def compute_step(tile, carry):
         slot = lax.rem(tile, 2)
@@ -464,28 +485,19 @@
         return carry
 
     def both_step(tile, carry):
-        near(tile)
-        far(tile)
+        near_and_far(tile, tile - 1)
         return carry
 
     def settle_step(tile, carry):
-        @pl.when(jnp.logical_not(middle))
-        def _():
-            settle(tile)
-
+        settle(tile, False)
         return carry
 
     def finish_step(tile, carry):
         finish(tile)
         return carry
 
-    def later_step(tile, carry):
-        @pl.when(jnp.logical_and(middle, tile < tiles))
-        def _():
-            near(tile)
-            far(tile)
-
-        settle_step(tile - 1, 0)
+    def inner_step(tile, carry):
+        near_and_far(tile, tile - 1)
         finish(tile - 1)
         return carry
 
@@ -493,33 +505,57 @@
         deliver(tile)
         return carry
 
-    def drain_step(tile, carry):
-        drain(tile)
+    def hops_step(tile, carry):
+        drain_hops(tile)
+        return carry
+
+    def send_step(tile, carry):
+        send_back(tile)
+        return carry
+
+    def back_step(tile, carry):
+        drain_back(tile)
         return carry
 
     lax.fori_loop(1, tiles, compute_step, 0)
     start_margins()
     lax.fori_loop(meet, jnp.where(middle, meet, tiles), near_step, 0)
-    lax.fori_loop(early, jnp.where(middle, meet + 1, early), both_step, 0)
+    if not early:
+
+        @pl.when(middle)
+        def _():
+            near(0)
+
+    first = max(early, 1)
+    lax.fori_loop(first, jnp.where(middle, meet + 1, first), both_step, 0)
 
     @pl.when(middle)
     def _():
         pass_margins(left_half)
-        near(meet + 1)
-        far(meet + 1)
+        near_and_far(meet + 1, meet)
         pass_margins(jnp.logical_not(left_half))
 
-    lax.fori_loop(0, meet, settle_step, 0)
+        lax.fori_loop(0, meet + 1, finish_step, 0)
+        lax.fori_loop(meet + 2, tiles, inner_step, 0)
+        far(tiles - 1)
+        finish(tiles - 1)
+        lax.fori_loop(0, tiles, deliver_step, 0)
+        lax.fori_loop(0, tiles, hops_step, 0)
 
     @pl.when(jnp.logical_not(middle))
     def _():
-        settle(meet)
+        lax.fori_loop(0, meet + 1, settle_step, 0)
         pass_margins(jnp.logical_not(left_half))
-
-    lax.fori_loop(0, meet + 1, finish_step, 0)
-    lax.fori_loop(meet + 2, tiles + 1, later_step, 0)
-    lax.fori_loop(0, jnp.where(middle, tiles, 0), deliver_step, 0)
-    lax.fori_loop(0, tiles, drain_step, 0)
+        lax.fori_loop(0, meet + 1, finish_step, 0)
+        held = max(tiles - 2, meet + 1)
+        lax.fori_loop(meet + 1, held, settle_step, 0)
+        lax.fori_loop(0, tiles, hops_step, 0)
+        lax.fori_loop(0, held, send_step, 0)
+        for tile in range(held, tiles):
+            settle(tile, True)
+        lax.fori_loop(meet + 1, tiles, finish_step, 0)
+        lax.fori_loop(0, tiles, back_step, 0)
+
     margin_copy(0, 0, 1, partner).wait_send()
 
     @pl.when(place < chips - 1)
@@ -543,12 +579,12 @@
     pieces = variants // TILE
     hbm = pl.BlockSpec(memory_space=pltpu.MemorySpace.HBM)
     vmem = pl.BlockSpec(memory_space=pltpu.MemorySpace.VMEM)
-    out = jax.ShapeDtypeStruct((rows, genes), jnp.float32)
+    held = pltpu.VMEM((rows, genes), jnp.float32)
     dma = pltpu.SemaphoreType.DMA
     f32 = jnp.float32
     return pl.pallas_call(
         functools.partial(kernel, chips, owners),
-        out_shape=(out, out),
+        out_shape=(held, held),
         in_specs=[hbm] * 4,
         out_specs=(vmem, vmem),
         scratch_shapes=[
@@ -577,7 +613,7 @@
             dma((3,)),
         ],
         compiler_params=pltpu.CompilerParams(
-            collective_id=0, has_side_effects=True, vmem_limit_bytes=67043328
+            collective_id=0, has_side_effects=True, vmem_limit_bytes=61 * 2**20
         ),
     )(hap_words, total_counts, allele_one, allele_two)
 

time: 115 us -> 110 us (0.957); the launches traced: 115 us -> 109 us
  Pallas kernels: 111 us -> 106 us
  local copies, waits for them, and re-layouts: 3.74 us -> 1.59 us
    pallas_call x1, Pallas kernels: 111 us -> 106 us  [per_device(): pl.pallas_call(functools.partial(kernel, chips, owners), out_shape=(held,...]
    unnamed x2, local copies, waits for them, and re-layouts: 3.74 us -> 1.59 us
where the time goes in v4:
time: 110 us; the launch traced here: 109 us
  Pallas kernels  106 us (96%)
  local copies, waits for them, and re-layouts  1.59 us (1%)
    pallas_call x1, Pallas kernels, per_device(): pl.pallas_call(functools.partial(kernel, chips, owners), out_shape=(held,...  106 us

profile of v4, /device:TPU:0, one launch (start us, length us, event | category | flops | bytes accessed | tf_op | source)
XLA Modules:
  0.0 108.7 jit_solution(6745651718213499375)
XLA Ops:
  0.6 106.5 %shard_map.59 = (f32[64,2048]{1,0:T(8,128)S(1)}, f32[64,2048]{1,0:T(8,128)S(1)}) custom-call(s32[2,64,128]{2,1,0:T(8,128)} %hap_ref.1, s32[1920,2048]{1,0:T(8,128)} %total_ref.1, s32[1920,2048]{1,0:T(8,128)} %one_ref.1, s32[1920,2048]{1,0:T(8,128)} %two_ref.1), custom_call_target="tpu_custom_call" | custom-call | tf_op jit(solution)/shard_map/pallas_call | solution.py:585
  107.1 0.8 copy.8
  107.9 0.8 copy.9

commit v5 on v4

--- a/solution.py
+++ b/solution.py
@@ -37,6 +37,8 @@
     word_send,
     word_recv,
     word_local,
+    block_send,
+    block_recv,
     in_sem,
     swap_send,
     swap_recv,
@@ -102,8 +104,6 @@
         pl.semaphore_signal(barrier, inc=1, device_id={"var": other}, device_id_type=MESH)
     inner = jnp.logical_and(place >= 2, place < chips - 2)
     greeted = jnp.where(middle, jnp.where(inner, 2, 1), chips // 2 - 2)
-    pl.semaphore_wait(barrier, owners + 1 + greeted)
-    local.wait()
 
     def peer(shift):
         other = group
@@ -124,9 +124,6 @@
 
     direct = [shift for shift in range(1, owners) if shift & (shift - 1) == 0]
     routed = [shift for shift in range(1, owners) if shift & (shift - 1) != 0]
-    for shift in direct:
-        word_copy(shift).start()
-
     def kinds(which):
         return pl.ds(which, 1 + which)
 
@@ -264,8 +261,9 @@
             hop_allelic(tile, rightward, step)
 
     def near(tile):
-        swap_copy(tile, 0).wait_recv()
-        swap_copy(tile, 1).wait_recv()
+        if not (isinstance(tile, int) and tile == 0):
+            swap_copy(tile, 0).wait_recv()
+            swap_copy(tile, 1).wait_recv()
         sweep_allelic(tile, left_half)
         sweep_total(tile, left_half)
 
@@ -280,11 +278,36 @@
         sweep_allelic(tile, jnp.logical_not(left_half))
         sweep_total(tile, jnp.logical_not(left_half))
 
-    def first_forward():
-        swap_copy(0, 0).wait_recv()
-        sweep_total(0, left_half)
-        swap_copy(0, 1).wait_recv()
-        sweep_allelic(0, left_half)
+    def block_swap(owner, which):
+        return pltpu.make_async_remote_copy(
+            src_ref=own.at[0, kinds(which), owner, 1 - core],
+            dst_ref=swapped.at[0, kinds(which), owner],
+            send_sem=block_send.at[owner, which],
+            recv_sem=block_recv.at[owner, which],
+            device_id={"samp": partner},
+            device_id_type=MESH,
+        )
+
+    def first_block(owner):
+        build_table(owner)
+        part = pl.ds(pl.multiple_of(owner * block, block), block)
+        for kind in range(3):
+            product = jnp.dot(
+                tables[kind, part, :], feats[kind], preferred_element_type=jnp.float32
+            )
+            own[0, kind, owner] = product.reshape(2, rows, TILE)
+            if kind != 1:
+                block_swap(owner, min(kind, 1)).start()
+
+    def first_hop(target, which):
+        block_swap(target, which).wait_recv()
+        ahead = jnp.where(left_half, target - place, place - target)
+        needed = jnp.where(left_half, target >= chips // 2, target < chips // 2)
+        last = jnp.logical_and(jnp.logical_not(left_half), ahead == 1)
+
+        @pl.when(needed if which else ahead > 0)
+        def _():
+            hop(0, target, left_half, which, False if which else last)
 
     def settle(tile, send):
         columns = pl.ds(pl.multiple_of(tile * TILE, TILE), TILE)
@@ -313,7 +336,11 @@
 
     def drain_hops(tile):
         for which in range(2):
-            swap_copy(tile, which).wait_send()
+
+            @pl.when(tile > 0)
+            def _():
+                swap_copy(tile, which).wait_send()
+
         for target in range(chips):
 
             @pl.when(target != place)
@@ -421,31 +448,46 @@
             / jnp.sqrt((dosage_var + 1.0) * (gene_var + 1.0))
         )
 
-    for shift in direct:
-        word_copy(shift).wait_send()
-    for shift in routed:
-        word_copy(shift).start()
     for copy in fetch(0, 0):
         copy.wait()
     if tiles > 1:
         for copy in fetch(1, 1):
             copy.start()
     compute_features(0, 0)
-    build_table(group)
-    for shift in direct + routed:
-        word_copy(shift).wait_recv()
-        build_table(peer(shift))
+    pl.semaphore_wait(barrier, owners + 1 + greeted)
+    local.wait()
+    for shift in direct:
+        word_copy(shift).start()
+
+    blocks = [0] + direct + routed
+    for index, shift in enumerate(blocks):
+        if shift:
+            word_copy(shift).wait_recv()
+        first_block(peer(shift))
+        if not shift:
+            for other in direct:
+                word_copy(other).wait_send()
+            for other in routed:
+                word_copy(other).start()
+
+        @pl.when(jnp.logical_not(middle))
+        def _():
+            if index:
+                first_hop(peer(blocks[index - 1]), 1)
+            first_hop(peer(shift), 0)
+
+    @pl.when(jnp.logical_not(middle))
+    def _():
+        first_hop(peer(blocks[-1]), 1)
+
+    @pl.when(middle)
+    def _():
+        for shift in blocks:
+            for which in range(2):
+                block_swap(peer(shift), which).wait_recv()
+
     for shift in routed:
         word_copy(shift).wait_send()
-    multiply(0, 0)
-    swap_copy(0, 0).start()
-    for kind in (1, 2):
-        multiply(0, kind)
-    swap_copy(0, 1).start()
-
-    @pl.when(jnp.logical_not(middle))
-    def _():
-        first_forward()
 
     sum_tables()
 
@@ -468,7 +510,13 @@
         for which in range(2):
             swap_copy(tile, which).start()
 
-        @pl.when(jnp.logical_and(jnp.logical_not(middle), jnp.logical_and(tile > 1, tile <= meet)))
+        if meet > 1:
+
+            @pl.when(jnp.logical_and(jnp.logical_not(middle), tile == 1))
+            def _():
+                near(tile)
+
+        @pl.when(jnp.logical_and(jnp.logical_not(middle), jnp.logical_and(tile > 2, tile <= meet)))
         def _():
             near(tile - 1)
 
@@ -556,6 +604,9 @@
         lax.fori_loop(meet + 1, tiles, finish_step, 0)
         lax.fori_loop(0, tiles, back_step, 0)
 
+    for shift in blocks:
+        for which in range(2):
+            block_swap(peer(shift), which).wait_send()
     margin_copy(0, 0, 1, partner).wait_send()
 
     @pl.when(place < chips - 1)
@@ -602,6 +653,8 @@
             dma((owners,)),
             dma((owners,)),
             dma,
+            dma((owners, 2)),
+            dma((owners, 2)),
             dma((2, 3)),
             dma((tiles, 2)),
             dma((tiles, 2)),

time: 110 us -> 108 us (0.982)
    pallas_call x1, Pallas kernels: 106 us -> 105 us  [per_device(): pl.pallas_call(functools.partial(kernel, chips, owners), out_shape=(held,...]
where the time goes in v5:
time: 108 us; the launch traced here: 107 us
  Pallas kernels  105 us (97%)
  local copies, waits for them, and re-layouts  1.59 us (1%)
    pallas_call x1, Pallas kernels, per_device(): pl.pallas_call(functools.partial(kernel, chips, owners), out_shape=(held,...  105 us

profile of v5, /device:TPU:0, one launch (start us, length us, event | category | flops | bytes accessed | tf_op | source)
XLA Modules:
  0.0 106.8 jit_solution(17718695124328449075)
XLA Ops:
  0.6 104.6 %shard_map.59 = (f32[64,2048]{1,0:T(8,128)S(1)}, f32[64,2048]{1,0:T(8,128)S(1)}) custom-call(s32[2,64,128]{2,1,0:T(8,128)} %hap_ref.1, s32[1920,2048]{1,0:T(8,128)} %total_ref.1, s32[1920,2048]{1,0:T(8,128)} %one_ref.1, s32[1920,2048]{1,0:T(8,128)} %two_ref.1), custom_call_target="tpu_custom_call" | custom-call | tf_op jit(solution)/shard_map/pallas_call | solution.py:636
  105.2 0.8 copy.8
  106.0 0.8 copy.9
